TPU v7x, 256 devices: a whole 4x4x8 slice. The times are simulated.
256 devices in a mesh: gx: 16 (over y, z_hi), gy: 8 (over x, core), gz: 2 (over z_lo).
Axes of the slice: x: 4, y: 4, z: 8 (z_hi: 4, z_lo: 2; z = z_hi * 2 + z_lo), core: 2. Of those that a mesh axis runs over, the one named last changes fastest.
Arguments:
- fraction: float32 [64, 1024, 1024], P('gx', 'gy', 'gz'), may hold values from 0 to 1
- orientation: int32 [64, 1024, 1024], P('gx', 'gy', 'gz'), may hold values from 0 to 2
- interface: int32 [64, 1024, 1024], P('gx', 'gy', 'gz'), may hold values from 0 to 1
Outputs:
- curvature: float32 [64, 1024, 1024], P('gx', 'gy', 'gz')
- peak: float32 [], replicated
All inputs are finite; a program needn't handle non-finite values.
Results may differ from a plain program's by a relative error of at most 0.0003.
Values sent between devices are 32-bit elements; how exact they have to be, the bound alone decides.
A program may use at most 64 MiB of HBM per device.

v0:
```python
import functools

import jax
import jax.numpy as jnp
from jax import lax
from jax.sharding import Mesh
from jax.sharding import PartitionSpec as P

GX_GY_GZ = ("gx_0", "gx_1", "gy_0", "gy_1", "gz")
GX = ("gx_0", "gx_1")
GY = ("gy_0", "gy_1")


def with_halo(array, sides, width):
    for axis, dim in sides:
        peers, length = (lax.axis_size(axis), array.shape[dim])
        up = [(i, (i + 1) % peers) for i in range(peers - 1)]
        down = [(j, i) for i, j in up]
        last = lax.slice_in_dim(array, length - width, length, axis=dim)
        first = lax.slice_in_dim(array, 0, width, axis=dim)
        before = lax.ppermute(last, axis, up)
        after = lax.ppermute(first, axis, down)
        array = jnp.concatenate([before, array, after], axis=dim)
    return array


def over_axes(array, axes):
    return functools.reduce(lax.pmax, axes, array)


def curvature_block(padded, orientation, interface):
    shape = orientation.shape
    results = []
    for axis in range(3):
        others = [other for other in range(3) if other != axis]
        column = lax.slice_in_dim(padded, 0, shape[axis], axis=axis)
        for step in range(1, 7):
            column = column + lax.slice_in_dim(padded, step, step + shape[axis], axis=axis)

        def height(first, second):
            starts = [3, 3, 3]
            starts[axis] = 0
            starts[others[0]] += first
            starts[others[1]] += second
            return lax.slice(column, starts, [st + sz for st, sz in zip(starts, shape)])

        centre = height(0, 0)
        plus_a, minus_a = (height(1, 0), height(-1, 0))
        plus_b, minus_b = (height(0, 1), height(0, -1))
        slope_a = 0.5 * (plus_a - minus_a)
        slope_b = 0.5 * (plus_b - minus_b)
        bend_a = plus_a - 2.0 * centre + minus_a
        bend_b = plus_b - 2.0 * centre + minus_b
        twist = 0.25 * (height(1, 1) - height(1, -1) - height(-1, 1) + height(-1, -1))
        numer = (
            bend_a * (1.0 + slope_b * slope_b)
            + bend_b * (1.0 + slope_a * slope_a)
            - 2.0 * twist * slope_a * slope_b
        )
        denom = 1.0 + slope_a * slope_a + slope_b * slope_b
        results.append(numer / (denom * jnp.sqrt(denom)))
    picked = jnp.where(
        orientation == 0, results[0], jnp.where(orientation == 1, results[1], results[2])
    )
    return jnp.where(interface == 1, picked, jnp.zeros_like(picked))


def body(fraction, orientation, interface):
    padded = with_halo(fraction, ((GX, 0), (GY, 1), ("gz", 2)), 3)
    curvature = curvature_block(padded, orientation, interface)
    peak = over_axes(jnp.max(jnp.abs(curvature)), GX_GY_GZ)
    return (curvature, peak)


def solution(mesh):
    torus = Mesh(
        mesh.devices.reshape(4, 4, 4, 2, mesh.shape["gz"]), ("gx_0", "gx_1", "gy_0", "gy_1", "gz")
    )
    in_specs = (P(GX, GY, "gz"), P(GX, GY, "gz"), P(GX, GY, "gz"))
    out_specs = (P(GX, GY, "gz"), P())
    return jax.shard_map(body, mesh=torus, in_specs=in_specs, out_specs=out_specs, check_vma=False)
```

profile of v0, /device:TPU:1, one launch (start us, length us, event | category | flops | bytes accessed | tf_op | source)
XLA Modules:
  0.0 174.5 jit_solution(13068366260597955910)
XLA Ops:
  0.6 1.5 fusion.21
  2.1 1.3 collective-permute-start.1
  3.4 6.4 %collective-permute-start = (f32[3,128,512]{2,1,0:T(8,128)S(1)}, f32[3,128,512]{2,1,0:T(8,128)S(1)}, u32[]{:S(2)}, u32[]{:S(2)}) collective-permute-start(f32[3,128,512]{2,1,0:T(8,128)S(1)} %get-tuple-element.16), channel_id=1, source_target_pairs={{0,16},{16,32},{32,48},{48,64},{64,80},{80,96},{96,112},{112,128},... | collective-permute-start | bytes 2359304 | tf_op jit(solution)/shard_map/ppermute | solution.py:21
  9.8 1.9 %copy.63 = f32[4,128,512]{2,0,1:T(4,128)S(1)} copy(f32[4,128,512]{2,1,0:T(8,128)} %param.3) | data formatting | bytes 2097152 | tf_op args[0]
  11.7 0.0 copy-start
  11.7 29.6 %collective-permute-done.1 = f32[3,128,512]{2,1,0:T(8,128)S(1)} collective-permute-done((f32[3,128,512]{2,1,0:T(8,128)S(1)}, f32[3,128,512]{2,1,0:T(8,128)S(1)}, u32[]{:S(2)}, u32[]{:S(2)}) %collective-permute-start.1) | collective-permute-done | bytes 786464 | tf_op jit(solution)/shard_map/ppermute | solution.py:22
  41.3 0.5 copy.64
  41.9 0.0 copy-start.2
  41.9 0.0 collective-permute-done
  41.9 0.5 copy.62
  42.5 0.0 copy-start.4
  42.5 0.1 pad_maximum_fusion.5
  42.5 3.8 %collective-permute-start.3 = (f32[10,3,512]{2,0,1:T(8,128)S(1)}, f32[10,3,512]{2,0,1:T(8,128)S(1)}, u32[]{:S(2)}, u32[]{:S(2)}) collective-permute-start(f32[10,3,512]{2,0,1:T(8,128)S(1)} %get-tuple-element.15), channel_id=1, source_target_pairs={{2,0},{4,2},{6,4},{8,6},{10,8},{12,10},{14,12},{3,1},{5,3},{7,5},{... | collective-permute-start | bytes 184328 | tf_op jit(solution)/shard_map/ppermute | solution.py:22
  46.3 3.0 %collective-permute-start.2 = (f32[10,3,512]{2,0,1:T(8,128)S(1)}, f32[10,3,512]{2,0,1:T(8,128)S(1)}, u32[]{:S(2)}, u32[]{:S(2)}) collective-permute-start(f32[10,3,512]{2,0,1:T(8,128)S(1)} %get-tuple-element.14), channel_id=1, source_target_pairs={{0,2},{2,4},{4,6},{6,8},{8,10},{10,12},{12,14},{1,3},{3,5},{5,7},{... | collective-permute-start | bytes 184328 | tf_op jit(solution)/shard_map/ppermute | solution.py:21
  49.3 0.4 collective-permute-done.3
  49.7 1.3 collective-permute-done.2
  50.9 1.1 pad_maximum_fusion.2
  52.0 1.8 %fusion.20 = (f32[10,134,3]{2,0,1:T(8,128)}, f32[10,134,3]{2,0,1:T(8,128)}) fusion(f32[10,134,512]{2,0,1:T(8,128)S(1)} %pad_maximum_fusion.2), kind=kLoop, calls=%fused_computation.60 | loop fusion | bytes 64320 | tf_op jit(solution)/shard_map/slice | solution.py:19
  53.8 1.9 %copy.65 = f32[10,134,3]{1,0,2:T(8,128)S(1)} copy(f32[10,134,3]{2,0,1:T(8,128)} %get-tuple-element.10) | data formatting | bytes 32160 | tf_op jit(solution)/shard_map/slice | solution.py:19
  55.7 3.9 %collective-permute-start.4 = (f32[10,134,3]{1,0,2:T(8,128)S(1)}, f32[10,134,3]{1,0,2:T(8,128)S(1)}, u32[]{:S(2)}, u32[]{:S(2)}) collective-permute-start(f32[10,134,3]{1,0,2:T(8,128)S(1)} %copy.65), channel_id=1, source_target_pairs={{0,1},{2,3},{4,5},{6,7},{8,9},{10,11},{12,13},{14,15},{16,17},{18,... | collective-permute-start | bytes 48248 | tf_op jit(solution)/shard_map/ppermute | solution.py:21
  59.6 1.9 %copy.66 = f32[10,134,3]{1,0,2:T(8,128)S(1)} copy(f32[10,134,3]{2,0,1:T(8,128)} %get-tuple-element.11) | data formatting | bytes 32160 | tf_op jit(solution)/shard_map/slice | solution.py:20
  61.5 1.5 collective-permute-start.5
  63.0 0.0 collective-permute-done.4
  63.0 1.7 copy.67
  64.7 1.6 collective-permute-done.5
  66.3 1.7 copy.68
  68.0 0.0 copy-done
  68.0 0.0 copy-done.2
  68.0 0.0 copy-done.4
  68.0 7.7 %pad_maximum_fusion = f32[10,134,518]{2,0,1:T(8,128)S(1)} fusion(f32[10,134,3]{2,0,1:T(8,128)} %copy.68, f32[10,3,512]{2,0,1:T(8,128)S(1)} %collective-permute-done.3, f32[3,128,512]{2,0,1:T(4,128)S(1)} %copy.64, f32[4,128,512]{2,0,1:T(4,128)S(1)} %copy.63, f32[3,128,512]{2,0,1:T(4,128)S(1)} %copy.62, f32[10,3,512]{2,0,1:T(8,128)S(1)} %collective-permute-done.2, ...), kind=kLoop, calls=%fused_computation | loop fusion | flops 4164720 | bytes 5552960 | tf_op jit(solution)/shard_map/concatenate | solution.py:23
  75.8 5.1 %slice_add_fusion = f32[10,128,518]{2,0,1:T(8,128)} fusion(f32[10,134,518]{2,0,1:T(8,128)S(1)} %pad_maximum_fusion), kind=kLoop, calls=%fused_computation.3 | loop fusion | flops 3978240 | bytes 21217280 | tf_op jit(solution)/shard_map/add | solution.py:38
  80.8 0.0 copy-start.1
  80.9 0.0 copy-start.3
  80.9 0.0 copy-start.5
  80.9 0.0 copy-start.6
  80.9 0.0 copy-start.7
  80.9 1.6 slice_add_fusion.11
  82.5 0.0 copy-done.1
  82.5 0.0 copy-done.3
  82.5 0.2 copy-done.5
  82.7 0.3 copy-done.6
  83.0 0.3 copy-done.7
  83.4 7.4 %maximum_maximum_fusion = (f32[10,134,515]{2,0,1:T(8,128)S(1)}, f32[10,134,515]{2,0,1:T(8,128)S(1)}) fusion(f32[10,3,512]{2,0,1:T(8,128)S(1)} %collective-permute-done.3, f32[3,128,512]{2,0,1:T(4,128)S(1)} %copy-done.3, f32[4,128,512]{2,0,1:T(4,128)S(1)} %copy-done.1, f32[3,128,512]{2,0,1:T(4,128)S(1)} %copy-done.5, ...), kind=kLoop, calls=%fused_computation.1 | loop fusion | flops 6901000 | bytes 8297280 | tf_op jit(solution)/shard_map/concatenate | solution.py:23
  90.8 8.8 %slice_add_fusion.6 = f32[10,134,512]{2,0,1:T(8,128)} fusion(f32[10,134,515]{2,0,1:T(8,128)S(1)} %get-tuple-element.13, f32[10,134,515]{2,0,1:T(8,128)S(1)} %get-tuple-element.12, f32[10,3,512]{2,0,1:T(8,128)S(1)} %collective-permute-done.3, f32[3,128,512]{2,0,1:T(4,128)} %copy-done.2, f32[4,128,512]{2,0,1:T(4,128)} %copy-done, f32[3,128,512]{2,0,1:T(4,128)} %copy-done.4, ...), kind=kLoop, calls=%fused_computation.9 | loop fusion | flops 6860800 | bytes 21954560 | tf_op jit(solution)/shard_map/add | solution.py:38
  99.6 24.3 %abs_reduce_fusion = (f32[]{:T(128)}, f32[4,128,512]{2,0,1:T(4,128)S(1)}) fusion(f32[10,134,512]{2,0,1:T(8,128)} %slice_add_fusion.6, f32[10,128,518]{2,0,1:T(8,128)} %slice_add_fusion, f32[4,134,518]{2,0,1:T(4,128)S(1)} %slice_add_fusion.11, s32[4,128,512]{2,1,0:T(8,128)} %param.4, s32[4,128,512]{2,1,0:T(8,128)} %param.5), kind=kLoop, calls=%fused_computation.55 | loop fusion | flops 22544384 | bytes 31457284 | tf_op jit(solution)/shard_map/reduce_max | solution.py:71
  123.9 17.1 %pmax.35 = f32[]{:T(128)} all-reduce(f32[]{:T(128)} %get-tuple-element.8), channel_id=1, replica_groups=mesh['gx_0'=4,'gx_1'=4,'gy_0'=4,'gy_1'=2,'gz'=2] {'gx_0'}, use_global_device_ids=true, to_apply=%region_1.2 | all-reduce | flops 1 | bytes 8 | tf_op jit(solution)/shard_map/pmax | solution.py:28
  141.0 7.5 %pmax.36 = f32[]{:T(128)} all-reduce(f32[]{:T(128)} %pmax.35), channel_id=1, replica_groups=mesh['gx_0'=4,'gx_1'=4,'gy_0'=4,'gy_1'=2,'gz'=2] {'gx_1'}, use_global_device_ids=true, to_apply=%region_2.3 | all-reduce | flops 1 | bytes 8 | tf_op jit(solution)/shard_map/pmax | solution.py:28
  148.5 8.0 %pmax.37 = f32[]{:T(128)} all-reduce(f32[]{:T(128)} %pmax.36), channel_id=1, replica_groups=mesh['gx_0'=4,'gx_1'=4,'gy_0'=4,'gy_1'=2,'gz'=2] {'gy_0'}, use_global_device_ids=true, to_apply=%region_3.4 | all-reduce | flops 1 | bytes 8 | tf_op jit(solution)/shard_map/pmax | solution.py:28
  156.4 12.4 %pmax.38 = f32[]{:T(128)} all-reduce(f32[]{:T(128)} %pmax.37), channel_id=1, replica_groups=mesh['gx_0'=4,'gx_1'=4,'gy_0'=4,'gy_1'=2,'gz'=2] {'gy_1'}, use_global_device_ids=true, to_apply=%region_4.5 | all-reduce | flops 1 | bytes 8 | tf_op jit(solution)/shard_map/pmax | solution.py:28
  168.8 1.3 copy.72
  170.1 4.4 %pmax.39 = f32[]{:T(128)} all-reduce(f32[]{:T(128)} %pmax.38), channel_id=1, replica_groups=mesh['gx_0'=4,'gx_1'=4,'gy_0'=4,'gy_1'=2,'gz'=2] {'gz'}, use_global_device_ids=true, to_apply=%region_5.6 | all-reduce | flops 1 | bytes 8 | tf_op jit(solution)/shard_map/pmax | solution.py:28
Async XLA Ops:
  2.1 39.2 %collective-permute-start.1 = (f32[3,128,512]{2,1,0:T(8,128)S(1)}, f32[3,128,512]{2,1,0:T(8,128)S(1)}, u32[]{:S(2)}, u32[]{:S(2)}) collective-permute-start(f32[3,128,512]{2,1,0:T(8,128)S(1)} %get-tuple-element.17), channel_id=1, source_target_pairs={{16,0},{32,16},{48,32},{64,48},{80,64},{96,80},{112,96},{128,112},... | collective-permute-start | bytes 2359304 | tf_op jit(solution)/shard_map/ppermute | solution.py:22
  3.4 38.5 %collective-permute-start = (f32[3,128,512]{2,1,0:T(8,128)S(1)}, f32[3,128,512]{2,1,0:T(8,128)S(1)}, u32[]{:S(2)}, u32[]{:S(2)}) collective-permute-start(f32[3,128,512]{2,1,0:T(8,128)S(1)} %get-tuple-element.16), channel_id=1, source_target_pairs={{0,16},{16,32},{32,48},{48,64},{64,80},{80,96},{96,112},{112,128},... | collective-permute-start | bytes 2359304 | tf_op jit(solution)/shard_map/ppermute | solution.py:21
  11.7 56.3 %copy-start = (f32[4,128,512]{2,0,1:T(4,128)}, f32[4,128,512]{2,0,1:T(4,128)S(1)}, u32[]{:S(2)}) copy-start(f32[4,128,512]{2,0,1:T(4,128)S(1)} %copy.63) | copy-start | bytes 3145732
  41.9 26.2 %copy-start.2 = (f32[3,128,512]{2,0,1:T(4,128)}, f32[3,128,512]{2,0,1:T(4,128)S(1)}, u32[]{:S(2)}) copy-start(f32[3,128,512]{2,0,1:T(4,128)S(1)} %copy.64) | copy-start | bytes 2359300
  42.5 25.6 %copy-start.4 = (f32[3,128,512]{2,0,1:T(4,128)}, f32[3,128,512]{2,0,1:T(4,128)S(1)}, u32[]{:S(2)}) copy-start(f32[3,128,512]{2,0,1:T(4,128)S(1)} %copy.62) | copy-start | bytes 2359300
  42.5 7.1 %collective-permute-start.3 = (f32[10,3,512]{2,0,1:T(8,128)S(1)}, f32[10,3,512]{2,0,1:T(8,128)S(1)}, u32[]{:S(2)}, u32[]{:S(2)}) collective-permute-start(f32[10,3,512]{2,0,1:T(8,128)S(1)} %get-tuple-element.15), channel_id=1, source_target_pairs={{2,0},{4,2},{6,4},{8,6},{10,8},{12,10},{14,12},{3,1},{5,3},{7,5},{... | collective-permute-start | bytes 184328 | tf_op jit(solution)/shard_map/ppermute | solution.py:22
  46.3 4.6 %collective-permute-start.2 = (f32[10,3,512]{2,0,1:T(8,128)S(1)}, f32[10,3,512]{2,0,1:T(8,128)S(1)}, u32[]{:S(2)}, u32[]{:S(2)}) collective-permute-start(f32[10,3,512]{2,0,1:T(8,128)S(1)} %get-tuple-element.14), channel_id=1, source_target_pairs={{0,2},{2,4},{4,6},{6,8},{8,10},{10,12},{12,14},{1,3},{3,5},{5,7},{... | collective-permute-start | bytes 184328 | tf_op jit(solution)/shard_map/ppermute | solution.py:21
  55.7 7.3 %collective-permute-start.4 = (f32[10,134,3]{1,0,2:T(8,128)S(1)}, f32[10,134,3]{1,0,2:T(8,128)S(1)}, u32[]{:S(2)}, u32[]{:S(2)}) collective-permute-start(f32[10,134,3]{1,0,2:T(8,128)S(1)} %copy.65), channel_id=1, source_target_pairs={{0,1},{2,3},{4,5},{6,7},{8,9},{10,11},{12,13},{14,15},{16,17},{18,... | collective-permute-start | bytes 48248 | tf_op jit(solution)/shard_map/ppermute | solution.py:21
  61.5 4.8 %collective-permute-start.5 = (f32[10,134,3]{1,0,2:T(8,128)S(1)}, f32[10,134,3]{1,0,2:T(8,128)S(1)}, u32[]{:S(2)}, u32[]{:S(2)}) collective-permute-start(f32[10,134,3]{1,0,2:T(8,128)S(1)} %copy.66), channel_id=1, source_target_pairs={{1,0},{3,2},{5,4},{7,6},{9,8},{11,10},{13,12},{15,14},{17,16},{19,... | collective-permute-start | bytes 48248 | tf_op jit(solution)/shard_map/ppermute | solution.py:22
  80.8 1.7 copy-start.1
  80.9 1.7 copy-start.3
  80.9 1.9 %copy-start.5 = (f32[3,128,512]{2,0,1:T(4,128)S(1)}, f32[3,128,512]{2,0,1:T(4,128)}, u32[]{:S(2)}) copy-start(f32[3,128,512]{2,0,1:T(4,128)} %copy-done.4) | copy-start | bytes 2359300
  80.9 2.2 %copy-start.6 = (f32[10,134,3]{2,0,1:T(8,128)S(1)}, f32[10,134,3]{2,0,1:T(8,128)}, u32[]{:S(2)}) copy-start(f32[10,134,3]{2,0,1:T(8,128)} %copy.67) | copy-start | bytes 48244
  80.9 2.5 %copy-start.7 = (f32[10,134,3]{2,0,1:T(8,128)S(1)}, f32[10,134,3]{2,0,1:T(8,128)}, u32[]{:S(2)}) copy-start(f32[10,134,3]{2,0,1:T(8,128)} %copy.68) | copy-start | bytes 48244
where the time goes:
time: 175 us; the launch traced here: 174 us
  other arithmetic  56.1 us (32%)
  blocking collectives  49.3 us (28%)
  waiting for transfers between devices  32.8 us (19%)
  starting transfers between devices  19.8 us (11%)
  local copies, waits for them, and re-layouts  15.6 us (9%)
    pmax x5, blocking collectives, over_axes(): return functools.reduce(lax.pmax, axes, array)  49.3 us
    ppermute x3, waiting for transfers between devices, with_halo(): after = lax.ppermute(first, axis, down)  31.6 us
    reduce_max x1, other arithmetic, body(): peak = over_axes(jnp.max(jnp.abs(curvature)), GX_GY_GZ)  24.3 us
    concatenate x3, other arithmetic, with_halo(): array = jnp.concatenate([before, array, after], axis=dim)  16.2 us
    add x3, other arithmetic, curvature_block(): column + lax.slice_in_dim(padded, step, step + shape[axis], axis=axis)  15.5 us
    ppermute x3, starting transfers between devices, with_halo(): before = lax.ppermute(last, axis, up)  13.3 us
    ppermute x3, starting transfers between devices, with_halo(): after = lax.ppermute(first, axis, down)  6.52 us
    slice x3, local copies, waits for them, and re-layouts, with_halo(): last = lax.slice_in_dim(array, length - width, length, axis=dim)  5.14 us
  transfers between devices with their start and end apart: 6, of which 4 were waited for; matrix products, arithmetic and copies ran while one was open for 3% of the time, Pallas kernels for 0%

commit v1 on v0

v1 whole, which is shorter than its diff:
```python
import functools

import jax
import jax.numpy as jnp
from jax import lax
from jax.experimental import pallas as pl
from jax.experimental.pallas import tpu as pltpu
from jax.sharding import PartitionSpec as P

MESH = pl.DeviceIdType.MESH
LANES = 128
Z_HI = 4


def shifted(tiles, rolled, shift, lane):
    count = len(rolled)
    out = []
    for t in range(tiles):
        if shift > 0:
            out.append(jnp.where(lane >= LANES - shift, rolled[(t + 1) % count], rolled[t]))
        else:
            out.append(jnp.where(lane < -shift, rolled[(t - 1) % count], rolled[t]))
    return out


def roll_all(tiles, shift):
    return [pltpu.roll(x, (-shift) % LANES, x.ndim - 1) for x in tiles]


def kernel(
    sizes, f_hbm, ori_hbm, itf_hbm, out_hbm, peak_ref,
    ext, c0, d0, s0, c2, ori, itf, res, zs, zr, vmax, r1, r2,
    load_sem, store_sem, xs, xr, ys, yr, y4s, y4r, yxs, yxr, zss, zrs, r1s, r1r, r2s, r2r,
):
    ngx, ngy, ngz, zhi = sizes
    gx, gy, gz = lax.axis_index("gx"), lax.axis_index("gy"), lax.axis_index("gz")
    other = 1 - gz
    planes, rows, lanes = f_hbm.shape
    nt = lanes // LANES
    nr = rows // 8
    has_lo, has_hi = gx > 0, gx < ngx - 1
    y_lo, y_hi = gy > 0, gy < ngy - 1
    top = 8 + rows

    loads = [
        pltpu.make_async_copy(
            f_hbm.at[:, :, pl.ds(t * LANES, LANES)], ext.at[pl.ds(3, 4), t, pl.ds(8, rows), :],
            load_sem.at[t])
        for t in range(nt)
    ]
    load_ori = pltpu.make_async_copy(ori_hbm, ori, load_sem.at[nt])
    load_itf = pltpu.make_async_copy(itf_hbm, itf, load_sem.at[nt + 1])
    for copy in loads:
        copy.start()
    load_ori.start()
    load_itf.start()

    @pl.when(jnp.logical_not(has_lo))
    def _():
        ext[0:3] = jnp.zeros((3, nt + 1, rows + 16, LANES), jnp.float32)

    @pl.when(jnp.logical_not(has_hi))
    def _():
        ext[7:10] = jnp.zeros((3, nt + 1, rows + 16, LANES), jnp.float32)

    @pl.when(jnp.logical_not(y_lo))
    def _():
        ext[:, :, 0:8] = jnp.zeros((10, nt + 1, 8, LANES), jnp.float32)

    @pl.when(jnp.logical_not(y_hi))
    def _():
        ext[:, :, top:top + 8] = jnp.zeros((10, nt + 1, 8, LANES), jnp.float32)

    ny = ngx // zhi
    y_at, z_at = gx // zhi, gx % zhi
    n1, n2 = zhi * ngz, ny * ngy
    me1 = z_at * ngz + gz
    me2 = y_at * ngy + gy

    def peer1(d):
        i = lax.rem(me1 + d, n1)
        return (y_at * zhi + i // ngz, gy, lax.rem(i, ngz))

    def peer2(d):
        i = lax.rem(me2 + d, n2)
        return ((i // ngy) * zhi + z_at, lax.rem(i, ngy), gz)

    barrier = pltpu.get_barrier_semaphore()

    def greet(device):
        pl.semaphore_signal(barrier, inc=1, device_id=device, device_id_type=MESH)

    cross_hi = jnp.logical_and(has_hi, z_at == zhi - 1)
    cross_lo = jnp.logical_and(has_lo, z_at == 0)

    @pl.when(cross_hi)
    def _():
        greet((gx + 1, gy, gz))
        greet((gx + 1, gy, other))

    @pl.when(cross_lo)
    def _():
        greet((gx - 1, gy, gz))
        greet((gx - 1, gy, other))

    for d in range(1, n1):
        greet(peer1(d))
    for d in range(1, n2):
        greet(peer2(d))

    for copy in loads:
        copy.wait()

    edge = jnp.where(gz == 0, nt - 1, 0)
    for p in range(4):
        turned = jnp.transpose(ext[3 + p, edge, 8:top, :])
        zs[p] = jnp.where(gz == 0, turned[LANES - 8:LANES], turned[0:8])
    vmax[...] = jnp.zeros_like(vmax)

    greeted = n1 - 1 + n2 - 1 + jnp.where(cross_hi, 2, 0) + jnp.where(cross_lo, 2, 0)
    pl.semaphore_wait(barrier, greeted)

    def remote(src, dst, send, recv, device):
        return pltpu.make_async_remote_copy(
            src_ref=src, dst_ref=dst, send_sem=send, recv_sem=recv, device_id=device,
            device_id_type=MESH)

    z_own = remote(zs, zr.at[pl.ds(3, 4)], zss.at[0], zrs.at[0], (gx, gy, other))
    z_up = remote(zs.at[pl.ds(1, 3)], zr.at[pl.ds(0, 3)], zss.at[1], zrs.at[1], (gx + 1, gy, other))
    z_dn = remote(zs.at[pl.ds(0, 3)], zr.at[pl.ds(7, 3)], zss.at[2], zrs.at[2], (gx - 1, gy, other))

    def x_up(r):
        at = pl.ds(pl.multiple_of(8 + r * 8, 8), 8)
        return remote(ext.at[pl.ds(4, 3), pl.ds(0, nt), at, :], ext.at[pl.ds(0, 3), pl.ds(0, nt), at, :],
                      xs.at[0, r], xr.at[0, r], (gx + 1, gy, gz))

    def x_dn(r):
        at = pl.ds(pl.multiple_of(8 + r * 8, 8), 8)
        return remote(ext.at[pl.ds(3, 3), pl.ds(0, nt), at, :], ext.at[pl.ds(7, 3), pl.ds(0, nt), at, :],
                      xs.at[1, r], xr.at[1, r], (gx - 1, gy, gz))

    def y_up(first, count, t0, tn, send, recv):
        return remote(ext.at[pl.ds(first, count), pl.ds(t0, tn), pl.ds(rows, 8), :],
                      ext.at[pl.ds(first, count), pl.ds(t0, tn), pl.ds(0, 8), :], send, recv,
                      (gx, gy + 1, gz))

    def y_dn(first, count, t0, tn, send, recv):
        return remote(ext.at[pl.ds(first, count), pl.ds(t0, tn), pl.ds(8, 8), :],
                      ext.at[pl.ds(first, count), pl.ds(t0, tn), pl.ds(top, 8), :], send, recv,
                      (gx, gy - 1, gz))

    y_own = (y_up(3, 4, 0, nt, ys.at[0], yr.at[0]), y_dn(3, 4, 0, nt, ys.at[1], yr.at[1]))
    y_edge = (y_up(0, 10, nt, 1, y4s.at[0], y4r.at[0]), y_dn(0, 10, nt, 1, y4s.at[1], y4r.at[1]))
    y_far = [
        (y_up(first, 3, 0, nt, yxs.at[0, s], yxr.at[0, s]), y_dn(first, 3, 0, nt, yxs.at[1, s], yxr.at[1, s]))
        for s, first in ((0, 0), (1, 7))
    ]

    z_own.start()

    @pl.when(has_hi)
    def _():
        z_up.start()
        x_up(0).start()
        x_up(nr - 1).start()

    @pl.when(has_lo)
    def _():
        z_dn.start()
        x_dn(0).start()
        x_dn(nr - 1).start()

    @pl.when(y_hi)
    def _():
        y_own[0].start()

    @pl.when(y_lo)
    def _():
        y_own[1].start()

    def send_row(r, carry):
        @pl.when(has_hi)
        def _():
            x_up(r).start()

        @pl.when(has_lo)
        def _():
            x_dn(r).start()

        return carry

    lax.fori_loop(1, nr - 1, send_row, 0)

    def take_z(first, count):
        for p in range(first, first + count):
            part = zr[p]
            zero = jnp.zeros_like(part)
            low, high = jnp.where(gz == 0, part, zero), jnp.where(gz == 0, zero, part)
            middle = jnp.zeros((LANES - 16, LANES), jnp.float32)
            ext[p, nt, 8:top, :] = jnp.transpose(jnp.concatenate([low, middle, high], axis=0))

    z_own.wait_recv()
    take_z(3, 4)

    @pl.when(has_lo)
    def _():
        z_up.wait_recv()
        take_z(0, 3)

    @pl.when(has_hi)
    def _():
        z_dn.wait_recv()
        take_z(7, 3)

    def arrived(r):
        @pl.when(has_lo)
        def _():
            x_up(r).wait_recv()

        @pl.when(has_hi)
        def _():
            x_dn(r).wait_recv()

    arrived(0)
    arrived(nr - 1)

    for ok, k in ((y_hi, 0), (y_lo, 1)):
        @pl.when(ok)
        def _(k=k):
            y_edge[k].start()

        @pl.when(jnp.logical_and(ok, has_lo))
        def _(k=k):
            y_far[0][k].start()

        @pl.when(jnp.logical_and(ok, has_hi))
        def _(k=k):
            y_far[1][k].start()

    lane = lax.broadcasted_iota(jnp.int32, (8, LANES), 1)

    def columns(tile):
        at = pl.ds(pl.multiple_of(tile * 8, 8), 8)
        sums = []
        for t in range(nt + 1):
            e = [ext[p, t, at, :] for p in range(10)]
            mid = (e[3] + e[4]) + (e[5] + e[6])
            lo2, hi2 = e[2] + e[1], e[7] + e[8]
            sums.append([mid + (lo2 + e[0]), mid + lo2 + e[7], mid + e[2] + hi2, mid + (hi2 + e[9])])
        for x in range(4):
            h = [sums[t][x] for t in range(nt + 1)]
            after = shifted(nt, roll_all(h, 1), 1, lane)
            before = shifted(nt, roll_all(h, -1), -1, lane)
            for t in range(nt):
                c0[x, t, at, :] = h[t]
                d0[x, t, at, :] = after[t] - before[t]
                s0[x, t, at, :] = after[t] + before[t] - 2.0 * h[t]
        for p in range(6):
            f = [ext[2 + p, t, at, :] for t in range(nt + 1)]
            pair = [a + b for a, b in zip(f, shifted(nt + 1, roll_all(f, 1), 1, lane))]
            quad = [a + b for a, b in zip(pair, shifted(nt + 1, roll_all(pair, 2), 2, lane))]
            back = shifted(nt, roll_all(quad, -3), -3, lane)
            for t in range(nt):
                c2[p, t, at, :] = back[t] + (quad[t] - f[t])

    def curve(tile):
        row = tile * 8
        own = pl.ds(pl.multiple_of(row - 8, 8), 8)
        at = pl.ds(pl.multiple_of(row, 8), 8)
        up, dn = pl.ds(row + 1, 8), pl.ds(row - 1, 8)
        col = []
        for p in range(6):
            parts = []
            for t in range(nt + 1):
                v = [ext[2 + p, t, pl.ds(row + k, 8), :] for k in range(-3, 4)]
                parts.append(((v[0] + v[1]) + (v[2] + v[3])) + ((v[4] + v[5]) + v[6]))
            after = shifted(nt, roll_all(parts, 1), 1, lane)
            before = shifted(nt, roll_all(parts, -1), -1, lane)
            col.append((parts, [a - b for a, b in zip(after, before)], [a + b for a, b in zip(after, before)]))
        best = vmax[...]
        for t in range(nt):
            across = pl.ds(t * LANES, LANES)
            for x in range(4):
                o = ori[x, own, across]
                is0, is1 = o == 0, o == 1

                def pick(a, b, c):
                    return jnp.where(is0, a, jnp.where(is1, b, c))

                h0 = c0[x, t, at, :]
                u0, w0 = c0[x, t, up, :], c0[x, t, dn, :]
                h1 = col[x + 1][0][t]
                u1, w1 = col[x + 2][0][t], col[x][0][t]
                h2 = c2[x + 1, t, at, :]
                u2, w2 = c2[x + 2, t, at, :], c2[x, t, at, :]
                b2u, b2w = c2[x + 1, t, up, :], c2[x + 1, t, dn, :]
                twist2 = (c2[x + 2, t, up, :] - c2[x + 2, t, dn, :]) - (c2[x, t, up, :] - c2[x, t, dn, :])
                centre = pick(h0, h1, h2)
                plus, minus = pick(u0, u1, u2), pick(w0, w1, w2)
                slope_a = 0.5 * (plus - minus)
                bend_a = plus + minus - 2.0 * centre
                slope_b = 0.5 * pick(d0[x, t, at, :], col[x + 1][1][t], b2u - b2w)
                bend_b = pick(s0[x, t, at, :], col[x + 1][2][t] - 2.0 * h1, b2u + b2w - 2.0 * h2)
                twist = pick(d0[x, t, up, :] - d0[x, t, dn, :], col[x + 2][1][t] - col[x][1][t], twist2)
                qa, qb = slope_a * slope_a, slope_b * slope_b
                numer = bend_a * (1.0 + qb) + bend_b * (1.0 + qa) - 0.5 * twist * (slope_a * slope_b)
                inv = lax.rsqrt(1.0 + qa + qb)
                kappa = jnp.where(itf[x, own, across] == 1, numer * (inv * inv * inv), 0.0)
                res[x, own, across] = kappa
                best = jnp.maximum(best, jnp.abs(kappa))
        vmax[...] = best

    def store(tile):
        own = pl.ds(pl.multiple_of(tile * 8 - 8, 8), 8)
        return pltpu.make_async_copy(res.at[:, own, :], out_hbm.at[:, own, :], store_sem.at[tile - 1])

    for ok, k in ((y_lo, 0), (y_hi, 1)):
        @pl.when(ok)
        def _(k=k):
            y_own[k].wait_recv()
            y_edge[k].wait_recv()

        @pl.when(jnp.logical_and(ok, has_lo))
        def _(k=k):
            y_far[0][k].wait_recv()

        @pl.when(jnp.logical_and(ok, has_hi))
        def _(k=k):
            y_far[1][k].wait_recv()

    load_ori.wait()
    load_itf.wait()

    def edges(i, carry):
        columns(i + jnp.where(i >= 2, nr - 2, 0))
        return carry

    lax.fori_loop(0, 4, edges, 0)

    def middle(tile, carry):
        arrived(tile - 1)
        columns(tile)
        curve(tile - 1)
        store(tile - 1).start()
        return carry

    lax.fori_loop(2, nr, middle, 0)

    def tail(tile, carry):
        curve(tile)
        store(tile).start()
        return carry

    lax.fori_loop(nr - 1, nr + 1, tail, 0)

    r1[me1] = jnp.max(vmax[...], axis=0, keepdims=True)

    def red1(d):
        return remote(r1.at[me1], r1.at[me1], r1s.at[d], r1r.at[d], peer1(d))

    def red2(d):
        return remote(r2.at[me2], r2.at[me2], r2s.at[d], r2r.at[d], peer2(d))

    def recv1(d):
        return remote(r1.at[lax.rem(me1 - d + n1, n1)], r1.at[lax.rem(me1 - d + n1, n1)], r1s.at[d], r1r.at[d], peer1(d))

    def recv2(d):
        return remote(r2.at[lax.rem(me2 - d + n2, n2)], r2.at[lax.rem(me2 - d + n2, n2)], r2s.at[d], r2r.at[d], peer2(d))

    for d in range(1, n1):
        red1(d).start()
    for d in range(1, n1):
        recv1(d).wait_recv()
    r2[me2] = jnp.max(r1[...], axis=0)
    for d in range(1, n2):
        red2(d).start()

    z_own.wait_send()

    def sent_row(r, carry):
        @pl.when(has_hi)
        def _():
            x_up(r).wait_send()

        @pl.when(has_lo)
        def _():
            x_dn(r).wait_send()

        store(r + 1).wait()
        return carry

    lax.fori_loop(0, nr, sent_row, 0)

    @pl.when(has_hi)
    def _():
        z_up.wait_send()

    @pl.when(has_lo)
    def _():
        z_dn.wait_send()

    for ok, k in ((y_hi, 0), (y_lo, 1)):
        @pl.when(ok)
        def _(k=k):
            y_own[k].wait_send()
            y_edge[k].wait_send()

        @pl.when(jnp.logical_and(ok, has_lo))
        def _(k=k):
            y_far[0][k].wait_send()

        @pl.when(jnp.logical_and(ok, has_hi))
        def _(k=k):
            y_far[1][k].wait_send()

    for d in range(1, n1):
        red1(d).wait_send()
    for d in range(1, n2):
        recv2(d).wait_recv()
    peak_ref[0, 0] = jnp.max(r2[...])
    for d in range(1, n2):
        red2(d).wait_send()


def block(sizes, fraction, orientation, interface):
    planes, rows, lanes = fraction.shape
    ngx, ngy, ngz, zhi = sizes
    nt, nr = lanes // LANES, rows // 8
    n1, n2 = zhi * ngz, (ngx // zhi) * ngy
    dma = pltpu.SemaphoreType.DMA
    f32 = jnp.float32
    curvature, peak = pl.pallas_call(
        functools.partial(kernel, sizes),
        out_shape=(
            jax.ShapeDtypeStruct(fraction.shape, f32),
            jax.ShapeDtypeStruct((1, 1), f32),
        ),
        in_specs=[pl.BlockSpec(memory_space=pl.ANY)] * 3,
        out_specs=(pl.BlockSpec(memory_space=pl.ANY), pl.BlockSpec(memory_space=pltpu.SMEM)),
        scratch_shapes=[
            pltpu.VMEM((10, nt + 1, rows + 16, LANES), f32),
            pltpu.VMEM((4, nt, rows + 16, LANES), f32),
            pltpu.VMEM((4, nt, rows + 16, LANES), f32),
            pltpu.VMEM((4, nt, rows + 16, LANES), f32),
            pltpu.VMEM((6, nt, rows + 16, LANES), f32),
            pltpu.VMEM((planes, rows, lanes), jnp.int32),
            pltpu.VMEM((planes, rows, lanes), jnp.int32),
            pltpu.VMEM((planes, rows, lanes), f32),
            pltpu.VMEM((4, 8, LANES), f32),
            pltpu.VMEM((10, 8, LANES), f32),
            pltpu.VMEM((8, LANES), f32),
            pltpu.VMEM((n1, 1, LANES), f32),
            pltpu.VMEM((n2, 1, LANES), f32),
            dma((nt + 2,)), dma((nr,)),
            dma((2, nr)), dma((2, nr)),
            dma((2,)), dma((2,)),
            dma((2,)), dma((2,)),
            dma((2, 2)), dma((2, 2)),
            dma((3,)), dma((3,)),
            dma((n1,)), dma((n1,)),
            dma((n2,)), dma((n2,)),
        ],
        compiler_params=pltpu.CompilerParams(
            collective_id=0, has_side_effects=True, vmem_limit_bytes=62 * 1024 * 1024
        ),
    )(fraction, orientation, interface)
    return curvature, peak.reshape(())


def solution(mesh):
    sizes = (mesh.shape["gx"], mesh.shape["gy"], mesh.shape["gz"], min(Z_HI, mesh.shape["gx"]))
    spec = P("gx", "gy", "gz")
    return jax.shard_map(
        functools.partial(block, sizes), mesh=mesh, in_specs=(spec,) * 3, out_specs=(spec, P()), check_vma=False
    )
```

time: 175 us -> 65.2 us (0.37)
  Pallas kernels: 0 us -> 60.4 us
  other arithmetic: 56.1 us -> 0 us
  blocking collectives: 49.3 us -> 0 us
  waiting for transfers between devices: 32.8 us -> 0 us
  starting transfers between devices: 19.8 us -> 0 us
  local copies, waits for them, and re-layouts: 15.6 us -> 2.26 us
    pallas_call x0 -> x1, Pallas kernels: none -> 60.4 us  [block(): pl.pallas_call(functools.partial(kernel, sizes), out_shape=(jax.ShapeDtyp...]
    pmax x5 -> x0, blocking collectives: 49.3 us -> none  [over_axes(): return functools.reduce(lax.pmax, axes, array)]
    ppermute x6 -> x0, waiting for transfers between devices: 32.8 us -> none  [the longest x3 31.6 us: with_halo(): after = lax.ppermute(first, axis, down)]
    reduce_max x1 -> x0, other arithmetic: 24.3 us -> none  [body(): peak = over_axes(jnp.max(jnp.abs(curvature)), GX_GY_GZ)]
    ppermute x6 -> x0, starting transfers between devices: 19.8 us -> none  [the longest x3 13.3 us: with_halo(): before = lax.ppermute(last, axis, up)]
    concatenate x3 -> x0, other arithmetic: 16.2 us -> none  [with_halo(): array = jnp.concatenate([before, array, after], axis=dim)]
    add x3 -> x0, other arithmetic: 15.5 us -> none  [curvature_block(): column + lax.slice_in_dim(padded, step, step + shape[axis], axis=axis)]
    slice x4 -> x0, local copies, waits for them, and re-layouts: 7.02 us -> none  [the longest x3 5.14 us: with_halo(): last = lax.slice_in_dim(array, length - width, length, axis=dim)]
  transfers between devices with their start and end apart: 6 -> 0, of which waited for: 4 -> 0; matrix products, arithmetic and copies ran while one was open for 3% -> 0% of each run, Pallas kernels for 0% -> 0%
where the time goes in v1:
time: 65.2 us; the launch traced here: 65 us
  Pallas kernels  60.4 us (93%)
  between operations  2.33 us (4%)
  local copies, waits for them, and re-layouts  2.26 us (3%)
    pallas_call x1, Pallas kernels, block(): pl.pallas_call(functools.partial(kernel, sizes), out_shape=(jax.ShapeDtyp...  60.4 us
    unnamed x1, local copies, waits for them, and re-layouts  2.26 us

profile of v1, /device:TPU:1, one launch (start us, length us, event | category | flops | bytes accessed | tf_op | source)
XLA Modules:
  0.0 65.0 jit_solution(7855337263807886896)
XLA Ops:
  0.6 60.4 %shard_map.50 = (f32[4,128,512]{2,1,0:T(8,128)}, f32[1,1]{1,0:T(1,128)}) custom-call(f32[4,128,512]{2,1,0:T(8,128)} %f_hbm.1, s32[4,128,512]{2,1,0:T(8,128)} %ori_hbm.1, s32[4,128,512]{2,1,0:T(8,128)} %itf_hbm.1), custom_call_target="tpu_custom_call" | custom-call | tf_op jit(solution)/shard_map/pallas_call | solution.py:432
  61.1 2.3 %copy.7 = f32[4,128,512]{2,1,0:T(8,128)} copy(f32[4,128,512]{2,1,0:T(8,128)} %get-tuple-element.8) | data formatting | bytes 2097152

commit v2 on v1

--- a/solution.py
+++ b/solution.py
@@ -28,9 +28,9 @@
 
 
 def kernel(
-    sizes, f_hbm, ori_hbm, itf_hbm, out_hbm, peak_ref,
-    ext, c0, d0, s0, c2, ori, itf, res, zs, zr, vmax, r1, r2,
-    load_sem, store_sem, xs, xr, ys, yr, y4s, y4r, yxs, yxr, zss, zrs, r1s, r1r, r2s, r2r,
+    sizes, f_hbm, ori_hbm, itf_hbm, res, peak_ref,
+    ext, c0, d0, s0, c2, ori, itf, zs, zr, zt, vmax, r1, r2,
+    load_sem, xs, xr, ys, yr, y4s, y4r, yxs, yxr, zss, zrs, r1s, r1r, r2s, r2r, tok,
 ):
     ngx, ngy, ngz, zhi = sizes
     gx, gy, gz = lax.axis_index("gx"), lax.axis_index("gy"), lax.axis_index("gz")
@@ -55,22 +55,6 @@
     load_ori.start()
     load_itf.start()
 
-    @pl.when(jnp.logical_not(has_lo))
-    def _():
-        ext[0:3] = jnp.zeros((3, nt + 1, rows + 16, LANES), jnp.float32)
-
-    @pl.when(jnp.logical_not(has_hi))
-    def _():
-        ext[7:10] = jnp.zeros((3, nt + 1, rows + 16, LANES), jnp.float32)
-
-    @pl.when(jnp.logical_not(y_lo))
-    def _():
-        ext[:, :, 0:8] = jnp.zeros((10, nt + 1, 8, LANES), jnp.float32)
-
-    @pl.when(jnp.logical_not(y_hi))
-    def _():
-        ext[:, :, top:top + 8] = jnp.zeros((10, nt + 1, 8, LANES), jnp.float32)
-
     ny = ngx // zhi
     y_at, z_at = gx // zhi, gx % zhi
     n1, n2 = zhi * ngz, ny * ngy
@@ -85,28 +69,52 @@
         i = lax.rem(me2 + d, n2)
         return ((i // ngy) * zhi + z_at, lax.rem(i, ngy), gz)
 
+    nx, x_at, core = ngy // 2, gy // 2, lax.rem(gy, 2)
+
+    def steps(n):
+        return (1, n - 1) if n > 2 else (1,) * (n - 1)
+
+    ring = [(y_at * zhi + lax.rem(z_at + d, zhi), gy, gz) for d in steps(zhi)]
+    ring += [(lax.rem(y_at + d, ny) * zhi + z_at, gy, gz) for d in steps(ny)]
+    ring += [(gx, lax.rem(x_at + d, nx) * 2 + core, gz) for d in steps(nx)]
+    ring += [(gx, gy, other), (gx, gy + 1 - 2 * core, gz)]
     barrier = pltpu.get_barrier_semaphore()
 
-    def greet(device):
-        pl.semaphore_signal(barrier, inc=1, device_id=device, device_id_type=MESH)
-
-    cross_hi = jnp.logical_and(has_hi, z_at == zhi - 1)
-    cross_lo = jnp.logical_and(has_lo, z_at == 0)
-
-    @pl.when(cross_hi)
-    def _():
-        greet((gx + 1, gy, gz))
-        greet((gx + 1, gy, other))
-
-    @pl.when(cross_lo)
-    def _():
-        greet((gx - 1, gy, gz))
-        greet((gx - 1, gy, other))
-
-    for d in range(1, n1):
-        greet(peer1(d))
-    for d in range(1, n2):
-        greet(peer2(d))
+    def tell(semaphore, device):
+        pl.semaphore_signal(semaphore, inc=1, device_id=device, device_id_type=MESH)
+
+    extra = (
+        (jnp.logical_and(has_hi, z_at == zhi - 1), (gx + 1, gy, gz)),
+        (jnp.logical_and(has_lo, z_at == 0), (gx - 1, gy, gz)),
+        (jnp.logical_and(y_hi, core == 1), (gx, gy + 1, gz)),
+        (jnp.logical_and(y_lo, core == 0), (gx, gy - 1, gz)),
+    )
+    for ok, device in extra:
+        @pl.when(ok)
+        def _(device=device):
+            tell(barrier, device)
+
+    for device in ring:
+        tell(barrier, device)
+    greeted = len(ring)
+    for ok, _ in extra:
+        greeted = greeted + jnp.where(ok, 1, 0)
+
+    @pl.when(jnp.logical_not(has_lo))
+    def _():
+        ext[0:3] = jnp.zeros((3, nt + 1, rows + 16, LANES), jnp.float32)
+
+    @pl.when(jnp.logical_not(has_hi))
+    def _():
+        ext[7:10] = jnp.zeros((3, nt + 1, rows + 16, LANES), jnp.float32)
+
+    @pl.when(jnp.logical_not(y_lo))
+    def _():
+        ext[:, :, 0:8] = jnp.zeros((10, nt + 1, 8, LANES), jnp.float32)
+
+    @pl.when(jnp.logical_not(y_hi))
+    def _():
+        ext[:, :, top:top + 8] = jnp.zeros((10, nt + 1, 8, LANES), jnp.float32)
 
     for copy in loads:
         copy.wait()
@@ -114,10 +122,12 @@
     edge = jnp.where(gz == 0, nt - 1, 0)
     for p in range(4):
         turned = jnp.transpose(ext[3 + p, edge, 8:top, :])
-        zs[p] = jnp.where(gz == 0, turned[LANES - 8:LANES], turned[0:8])
+        part = jnp.where(gz == 0, turned[LANES - 3:LANES], turned[0:3])
+        for c in range(3):
+            zs[p, c] = part[c:c + 1]
+    zt[...] = jnp.zeros_like(zt)
     vmax[...] = jnp.zeros_like(vmax)
 
-    greeted = n1 - 1 + n2 - 1 + jnp.where(cross_hi, 2, 0) + jnp.where(cross_lo, 2, 0)
     pl.semaphore_wait(barrier, greeted)
 
     def remote(src, dst, send, recv, device):
@@ -125,9 +135,16 @@
             src_ref=src, dst_ref=dst, send_sem=send, recv_sem=recv, device_id=device,
             device_id_type=MESH)
 
+    nearest = 2 * gz
     z_own = remote(zs, zr.at[pl.ds(3, 4)], zss.at[0], zrs.at[0], (gx, gy, other))
-    z_up = remote(zs.at[pl.ds(1, 3)], zr.at[pl.ds(0, 3)], zss.at[1], zrs.at[1], (gx + 1, gy, other))
-    z_dn = remote(zs.at[pl.ds(0, 3)], zr.at[pl.ds(7, 3)], zss.at[2], zrs.at[2], (gx - 1, gy, other))
+    z_up = (
+        remote(zr.at[6], zr.at[2], zss.at[1], zrs.at[1], (gx + 1, gy, gz)),
+        remote(zr.at[pl.ds(4, 2), nearest], zr.at[pl.ds(0, 2), nearest], zss.at[2], zrs.at[2], (gx + 1, gy, gz)),
+    )
+    z_dn = (
+        remote(zr.at[3], zr.at[7], zss.at[3], zrs.at[3], (gx - 1, gy, gz)),
+        remote(zr.at[pl.ds(4, 2), nearest], zr.at[pl.ds(8, 2), nearest], zss.at[4], zrs.at[4], (gx - 1, gy, gz)),
+    )
 
     def x_up(r):
         at = pl.ds(pl.multiple_of(8 + r * 8, 8), 8)
@@ -150,9 +167,9 @@
                       (gx, gy - 1, gz))
 
     y_own = (y_up(3, 4, 0, nt, ys.at[0], yr.at[0]), y_dn(3, 4, 0, nt, ys.at[1], yr.at[1]))
-    y_edge = (y_up(0, 10, nt, 1, y4s.at[0], y4r.at[0]), y_dn(0, 10, nt, 1, y4s.at[1], y4r.at[1]))
+    y_edge = (y_up(3, 4, nt, 1, y4s.at[0], y4r.at[0]), y_dn(3, 4, nt, 1, y4s.at[1], y4r.at[1]))
     y_far = [
-        (y_up(first, 3, 0, nt, yxs.at[0, s], yxr.at[0, s]), y_dn(first, 3, 0, nt, yxs.at[1, s], yxr.at[1, s]))
+        (y_up(first, 3, 0, nt + 1, yxs.at[0, s], yxr.at[0, s]), y_dn(first, 3, 0, nt + 1, yxs.at[1, s], yxr.at[1, s]))
         for s, first in ((0, 0), (1, 7))
     ]
 
@@ -160,13 +177,11 @@
 
     @pl.when(has_hi)
     def _():
-        z_up.start()
         x_up(0).start()
         x_up(nr - 1).start()
 
     @pl.when(has_lo)
     def _():
-        z_dn.start()
         x_dn(0).start()
         x_dn(nr - 1).start()
 
@@ -189,28 +204,51 @@
 
         return carry
 
-    lax.fori_loop(1, nr - 1, send_row, 0)
-
-    def take_z(first, count):
+    first_rows = min(3, nr - 1)
+    lax.fori_loop(1, first_rows, send_row, 0)
+    for device in ring:
+        tell(tok.at[0], device)
+
+    def take_z(first, count, near):
         for p in range(first, first + count):
-            part = zr[p]
+            if near is None or p == near:
+                for c in range(3):
+                    zt[p, pl.ds(5 * gz + c, 1), :] = zr[p, c]
+            else:
+                zt[p, pl.ds(5 * gz + nearest, 1), :] = zr[p, nearest]
+        for p in range(first, first + count):
+            part = zt[p]
             zero = jnp.zeros_like(part)
             low, high = jnp.where(gz == 0, part, zero), jnp.where(gz == 0, zero, part)
-            middle = jnp.zeros((LANES - 16, LANES), jnp.float32)
-            ext[p, nt, 8:top, :] = jnp.transpose(jnp.concatenate([low, middle, high], axis=0))
+            between = jnp.zeros((LANES - 16, LANES), jnp.float32)
+            ext[p, nt, 8:top, :] = jnp.transpose(jnp.concatenate([low, between, high], axis=0))
 
     z_own.wait_recv()
-    take_z(3, 4)
+
+    @pl.when(has_hi)
+    def _():
+        z_up[0].start()
+        z_up[1].start()
 
     @pl.when(has_lo)
     def _():
-        z_up.wait_recv()
-        take_z(0, 3)
+        z_dn[0].start()
+        z_dn[1].start()
+
+    lax.fori_loop(first_rows, nr - 1, send_row, 0)
+    take_z(3, 4, None)
+
+    @pl.when(has_lo)
+    def _():
+        z_up[0].wait_recv()
+        z_up[1].wait_recv()
+        take_z(0, 3, 2)
 
     @pl.when(has_hi)
     def _():
-        z_dn.wait_recv()
-        take_z(7, 3)
+        z_dn[0].wait_recv()
+        z_dn[1].wait_recv()
+        take_z(7, 3, 7)
 
     def arrived(r):
         @pl.when(has_lo)
@@ -310,10 +348,6 @@
                 best = jnp.maximum(best, jnp.abs(kappa))
         vmax[...] = best
 
-    def store(tile):
-        own = pl.ds(pl.multiple_of(tile * 8 - 8, 8), 8)
-        return pltpu.make_async_copy(res.at[:, own, :], out_hbm.at[:, own, :], store_sem.at[tile - 1])
-
     for ok, k in ((y_lo, 0), (y_hi, 1)):
         @pl.when(ok)
         def _(k=k):
@@ -338,17 +372,26 @@
     lax.fori_loop(0, 4, edges, 0)
 
     def middle(tile, carry):
+        level = tile - 2
+
+        @pl.when(level < tok.shape[0])
+        def _():
+            pl.semaphore_wait(tok.at[level], len(ring))
+
+        @pl.when(level < tok.shape[0] - 1)
+        def _():
+            for device in ring:
+                tell(tok.at[level + 1], device)
+
         arrived(tile - 1)
         columns(tile)
         curve(tile - 1)
-        store(tile - 1).start()
         return carry
 
     lax.fori_loop(2, nr, middle, 0)
 
     def tail(tile, carry):
         curve(tile)
-        store(tile).start()
         return carry
 
     lax.fori_loop(nr - 1, nr + 1, tail, 0)
@@ -386,18 +429,19 @@
         def _():
             x_dn(r).wait_send()
 
-        store(r + 1).wait()
         return carry
 
     lax.fori_loop(0, nr, sent_row, 0)
 
     @pl.when(has_hi)
     def _():
-        z_up.wait_send()
+        z_up[0].wait_send()
+        z_up[1].wait_send()
 
     @pl.when(has_lo)
     def _():
-        z_dn.wait_send()
+        z_dn[0].wait_send()
+        z_dn[1].wait_send()
 
     for ok, k in ((y_hi, 0), (y_lo, 1)):
         @pl.when(ok)
@@ -417,9 +461,21 @@
         red1(d).wait_send()
     for d in range(1, n2):
         recv2(d).wait_recv()
-    peak_ref[0, 0] = jnp.max(r2[...])
+    peak_ref[...] = jnp.max(r2[...], axis=0)
     for d in range(1, n2):
         red2(d).wait_send()
+
+
+def settle(res, peak, out, peak_out, top, sems):
+    copies = [pltpu.make_async_copy(res.at[p], out.at[p], sems.at[p]) for p in range(res.shape[0])]
+    for copy in copies:
+        copy.start()
+    top[0, 0] = jnp.max(peak[...])
+    last = pltpu.make_async_copy(top, peak_out, sems.at[res.shape[0]])
+    last.start()
+    last.wait()
+    for copy in copies:
+        copy.wait()
 
 
 def block(sizes, fraction, orientation, interface):
@@ -427,16 +483,17 @@
     ngx, ngy, ngz, zhi = sizes
     nt, nr = lanes // LANES, rows // 8
     n1, n2 = zhi * ngz, (ngx // zhi) * ngy
+    hops = ngy // 4 + ngx // zhi // 2 + 1
     dma = pltpu.SemaphoreType.DMA
     f32 = jnp.float32
     curvature, peak = pl.pallas_call(
         functools.partial(kernel, sizes),
         out_shape=(
             jax.ShapeDtypeStruct(fraction.shape, f32),
-            jax.ShapeDtypeStruct((1, 1), f32),
+            jax.ShapeDtypeStruct((1, LANES), f32),
         ),
         in_specs=[pl.BlockSpec(memory_space=pl.ANY)] * 3,
-        out_specs=(pl.BlockSpec(memory_space=pl.ANY), pl.BlockSpec(memory_space=pltpu.SMEM)),
+        out_specs=(pl.BlockSpec(memory_space=pltpu.VMEM), pl.BlockSpec(memory_space=pltpu.VMEM)),
         scratch_shapes=[
             pltpu.VMEM((10, nt + 1, rows + 16, LANES), f32),
             pltpu.VMEM((4, nt, rows + 16, LANES), f32),
@@ -445,25 +502,36 @@
             pltpu.VMEM((6, nt, rows + 16, LANES), f32),
             pltpu.VMEM((planes, rows, lanes), jnp.int32),
             pltpu.VMEM((planes, rows, lanes), jnp.int32),
-            pltpu.VMEM((planes, rows, lanes), f32),
-            pltpu.VMEM((4, 8, LANES), f32),
+            pltpu.VMEM((4, 3, 1, LANES), f32),
+            pltpu.VMEM((10, 3, 1, LANES), f32),
             pltpu.VMEM((10, 8, LANES), f32),
             pltpu.VMEM((8, LANES), f32),
             pltpu.VMEM((n1, 1, LANES), f32),
             pltpu.VMEM((n2, 1, LANES), f32),
-            dma((nt + 2,)), dma((nr,)),
+            dma((nt + 2,)),
             dma((2, nr)), dma((2, nr)),
             dma((2,)), dma((2,)),
             dma((2,)), dma((2,)),
             dma((2, 2)), dma((2, 2)),
-            dma((3,)), dma((3,)),
+            dma((5,)), dma((5,)),
             dma((n1,)), dma((n1,)),
             dma((n2,)), dma((n2,)),
+            pltpu.SemaphoreType.REGULAR((hops - 1,)),
         ],
         compiler_params=pltpu.CompilerParams(
-            collective_id=0, has_side_effects=True, vmem_limit_bytes=62 * 1024 * 1024
+            collective_id=0, has_side_effects=True, vmem_limit_bytes=55000000
         ),
     )(fraction, orientation, interface)
+    curvature, peak = pl.pallas_call(
+        settle,
+        out_shape=(
+            jax.ShapeDtypeStruct(fraction.shape, f32),
+            jax.ShapeDtypeStruct((1, 1), f32),
+        ),
+        in_specs=[pl.BlockSpec(memory_space=pltpu.VMEM), pl.BlockSpec(memory_space=pltpu.VMEM)],
+        out_specs=(pl.BlockSpec(memory_space=pl.ANY),) * 2,
+        scratch_shapes=[pltpu.SMEM((1, 1), f32), dma((planes + 1,))], compiler_params=pltpu.CompilerParams(vmem_limit_bytes=1048576 * 2),
+    )(curvature, peak)
     return curvature, peak.reshape(())
 
 

time: 65.2 us -> 62 us (0.951)
  local copies, waits for them, and re-layouts: 2.26 us -> 0 us
  between operations: 2.33 us -> 0.64 us
  Pallas kernels: 60.4 us -> 61.2 us
    unnamed x1 -> x0, local copies, waits for them, and re-layouts: 2.26 us -> none
    pallas_call x0 -> x1, Pallas kernels: none -> 1.01 us  [block(): pl.pallas_call(settle, out_shape=(jax.ShapeDtypeStruct(fraction.shape, f3...]
where the time goes in v2:
time: 62 us; the launch traced here: 61.9 us
  Pallas kernels  61.2 us (99%)
  between operations  0.64 us (1%)
    pallas_call x1, Pallas kernels, block(): pl.pallas_call(functools.partial(kernel, sizes), out_shape=(jax.ShapeDtyp...  60.2 us

profile of v2, /device:TPU:1, one launch (start us, length us, event | category | flops | bytes accessed | tf_op | source)
XLA Modules:
  0.0 61.9 jit_solution(14726186477230189388)
XLA Ops:
  0.6 60.2 %shard_map.50 = (f32[4,128,512]{2,1,0:T(8,128)S(1)}, f32[1,128]{1,0:T(1,128)S(1)}) custom-call(f32[4,128,512]{2,1,0:T(8,128)} %f_hbm.1, s32[4,128,512]{2,1,0:T(8,128)} %ori_hbm.1, s32[4,128,512]{2,1,0:T(8,128)} %itf_hbm.1), custom_call_target="tpu_custom_call" | custom-call | tf_op jit(solution)/shard_map/pallas_call | solution.py:489
  60.9 1.0 %shard_map.51 = (f32[4,128,512]{2,1,0:T(8,128)}, f32[1,1]{1,0:T(1,128)}) custom-call(f32[4,128,512]{2,1,0:T(8,128)S(1)} %get-tuple-element.6.res, f32[1,128]{1,0:T(1,128)S(1)} %get-tuple-element.7.peak), custom_call_target="tpu_custom_call" | custom-call | tf_op jit(solution)/shard_map/pallas_call | solution.py:525

commit v3 on v2

--- a/solution.py
+++ b/solution.py
@@ -55,21 +55,27 @@
     load_ori.start()
     load_itf.start()
 
-    ny = ngx // zhi
+    ny, nx = ngx // zhi, ngy // 2
     y_at, z_at = gx // zhi, gx % zhi
-    n1, n2 = zhi * ngz, ny * ngy
-    me1 = z_at * ngz + gz
-    me2 = y_at * ngy + gy
-
-    def peer1(d):
-        i = lax.rem(me1 + d, n1)
-        return (y_at * zhi + i // ngz, gy, lax.rem(i, ngz))
-
-    def peer2(d):
-        i = lax.rem(me2 + d, n2)
-        return ((i // ngy) * zhi + z_at, lax.rem(i, ngy), gz)
-
-    nx, x_at, core = ngy // 2, gy // 2, lax.rem(gy, 2)
+    x_at, core = gy // 2, lax.rem(gy, 2)
+    n1, n2 = ny * ngy, zhi * ngz
+    me1, me2 = y_at * ngy + gy, z_at * ngz + gz
+
+    def around(d, n):
+        return min(d, n - d)
+
+    steps1 = [(dy, dx, dc) for dy in range(ny) for dx in range(nx) for dc in range(2)][1:]
+    steps1.sort(key=lambda d: (-around(d[0], ny) - around(d[1], nx), -d[2]))
+    steps2 = sorted(range(1, n2), key=lambda d: -around(d, n2))
+
+    def peer1(step, sign):
+        dy, dx, dc = step
+        y = lax.rem(y_at + sign * dy + ny, ny)
+        x = lax.rem(x_at + sign * dx + nx, nx)
+        return y, x * 2 + (1 - core if dc else core)
+
+    def peer2(d, sign):
+        return lax.rem(me2 + sign * d + n2, n2)
 
     def steps(n):
         return (1, n - 1) if n > 2 else (1,) * (n - 1)
@@ -204,7 +210,7 @@
 
         return carry
 
-    first_rows = min(3, nr - 1)
+    first_rows = 1
     lax.fori_loop(1, first_rows, send_row, 0)
     for device in ring:
         tell(tok.at[0], device)
@@ -398,24 +404,22 @@
 
     r1[me1] = jnp.max(vmax[...], axis=0, keepdims=True)
 
-    def red1(d):
-        return remote(r1.at[me1], r1.at[me1], r1s.at[d], r1r.at[d], peer1(d))
-
-    def red2(d):
-        return remote(r2.at[me2], r2.at[me2], r2s.at[d], r2r.at[d], peer2(d))
-
-    def recv1(d):
-        return remote(r1.at[lax.rem(me1 - d + n1, n1)], r1.at[lax.rem(me1 - d + n1, n1)], r1s.at[d], r1r.at[d], peer1(d))
-
-    def recv2(d):
-        return remote(r2.at[lax.rem(me2 - d + n2, n2)], r2.at[lax.rem(me2 - d + n2, n2)], r2s.at[d], r2r.at[d], peer2(d))
-
-    for d in range(1, n1):
+    def red1(k, sign=1):
+        y, at = peer1(steps1[k], sign)
+        slot = me1 if sign > 0 else y * ngy + at
+        return remote(r1.at[slot], r1.at[slot], r1s.at[k], r1r.at[k], (y * zhi + z_at, at, gz))
+
+    def red2(k, sign=1):
+        i = peer2(steps2[k], sign)
+        slot = me2 if sign > 0 else i
+        return remote(r2.at[slot], r2.at[slot], r2s.at[k], r2r.at[k], (y_at * zhi + i // ngz, gy, lax.rem(i, ngz)))
+
+    for d in range(n1 - 1):
         red1(d).start()
-    for d in range(1, n1):
-        recv1(d).wait_recv()
+    for d in range(n1 - 1):
+        red1(d, -1).wait_recv()
     r2[me2] = jnp.max(r1[...], axis=0)
-    for d in range(1, n2):
+    for d in range(n2 - 1):
         red2(d).start()
 
     z_own.wait_send()
@@ -457,12 +461,12 @@
         def _(k=k):
             y_far[1][k].wait_send()
 
-    for d in range(1, n1):
+    for d in range(n1 - 1):
         red1(d).wait_send()
-    for d in range(1, n2):
-        recv2(d).wait_recv()
+    for d in range(n2 - 1):
+        red2(d, -1).wait_recv()
     peak_ref[...] = jnp.max(r2[...], axis=0)
-    for d in range(1, n2):
+    for d in range(n2 - 1):
         red2(d).wait_send()
 
 
@@ -482,7 +486,7 @@
     planes, rows, lanes = fraction.shape
     ngx, ngy, ngz, zhi = sizes
     nt, nr = lanes // LANES, rows // 8
-    n1, n2 = zhi * ngz, (ngx // zhi) * ngy
+    n1, n2 = (ngx // zhi) * ngy, zhi * ngz
     hops = ngy // 4 + ngx // zhi // 2 + 1
     dma = pltpu.SemaphoreType.DMA
     f32 = jnp.float32

time: 62 us -> 59 us (0.952)
  Pallas kernels: 61.2 us -> 58.2 us
    pallas_call x1, Pallas kernels: 60.2 us -> 57.2 us  [block(): pl.pallas_call(functools.partial(kernel, sizes), out_shape=(jax.ShapeDtyp...]
where the time goes in v3:
time: 59 us; the launch traced here: 58.9 us
  Pallas kernels  58.2 us (99%)
  between operations  0.64 us (1%)
    pallas_call x1, Pallas kernels, block(): pl.pallas_call(functools.partial(kernel, sizes), out_shape=(jax.ShapeDtyp...  57.2 us

profile of v3, /device:TPU:1, one launch (start us, length us, event | category | flops | bytes accessed | tf_op | source)
XLA Modules:
  0.0 58.9 jit_solution(16430925147684613607)
XLA Ops:
  0.6 57.2 %shard_map.50 = (f32[4,128,512]{2,1,0:T(8,128)S(1)}, f32[1,128]{1,0:T(1,128)S(1)}) custom-call(f32[4,128,512]{2,1,0:T(8,128)} %f_hbm.1, s32[4,128,512]{2,1,0:T(8,128)} %ori_hbm.1, s32[4,128,512]{2,1,0:T(8,128)} %itf_hbm.1), custom_call_target="tpu_custom_call" | custom-call | tf_op jit(solution)/shard_map/pallas_call | solution.py:493
  57.9 1.0 %shard_map.51 = (f32[4,128,512]{2,1,0:T(8,128)}, f32[1,1]{1,0:T(1,128)}) custom-call(f32[4,128,512]{2,1,0:T(8,128)S(1)} %get-tuple-element.6.res, f32[1,128]{1,0:T(1,128)S(1)} %get-tuple-element.7.peak), custom_call_target="tpu_custom_call" | custom-call | tf_op jit(solution)/shard_map/pallas_call | solution.py:529

commit v4 on v3

--- a/solution.py
+++ b/solution.py
@@ -50,11 +50,6 @@
     ]
     load_ori = pltpu.make_async_copy(ori_hbm, ori, load_sem.at[nt])
     load_itf = pltpu.make_async_copy(itf_hbm, itf, load_sem.at[nt + 1])
-    for copy in loads:
-        copy.start()
-    load_ori.start()
-    load_itf.start()
-
     ny, nx = ngx // zhi, ngy // 2
     y_at, z_at = gx // zhi, gx % zhi
     x_at, core = gy // 2, lax.rem(gy, 2)
@@ -102,6 +97,10 @@
 
     for device in ring:
         tell(barrier, device)
+    for copy in loads:
+        copy.start()
+    load_ori.start()
+    load_itf.start()
     greeted = len(ring)
     for ok, _ in extra:
         greeted = greeted + jnp.where(ok, 1, 0)
@@ -212,8 +211,14 @@
 
     first_rows = 1
     lax.fori_loop(1, first_rows, send_row, 0)
-    for device in ring:
-        tell(tok.at[0], device)
+    def pass_on(level):
+        if level > 0 and level <= tok.shape[0]:
+            pl.semaphore_wait(tok.at[level - 1], len(ring))
+        if level < tok.shape[0]:
+            for device in ring:
+                tell(tok.at[level], device)
+
+    pass_on(0)
 
     def take_z(first, count, near):
         for p in range(first, first + count):
@@ -243,6 +248,7 @@
 
     lax.fori_loop(first_rows, nr - 1, send_row, 0)
     take_z(3, 4, None)
+    pass_on(1)
 
     @pl.when(has_lo)
     def _():
@@ -281,6 +287,7 @@
         def _(k=k):
             y_far[1][k].start()
 
+    pass_on(2)
     lane = lax.broadcasted_iota(jnp.int32, (8, LANES), 1)
 
     def columns(tile):
@@ -368,6 +375,7 @@
         def _(k=k):
             y_far[1][k].wait_recv()
 
+    pass_on(3)
     load_ori.wait()
     load_itf.wait()
 
@@ -376,19 +384,9 @@
         return carry
 
     lax.fori_loop(0, 4, edges, 0)
+    pass_on(4)
 
     def middle(tile, carry):
-        level = tile - 2
-
-        @pl.when(level < tok.shape[0])
-        def _():
-            pl.semaphore_wait(tok.at[level], len(ring))
-
-        @pl.when(level < tok.shape[0] - 1)
-        def _():
-            for device in ring:
-                tell(tok.at[level + 1], device)
-
         arrived(tile - 1)
         columns(tile)
         curve(tile - 1)

time: 59 us -> 58.8 us (level)
  no operation moved by 1% of the time
where the time goes in v4:
time: 58.8 us; the launch traced here: 58.7 us
  Pallas kernels  58 us (99%)
  between operations  0.64 us (1%)
    pallas_call x1, Pallas kernels, block(): pl.pallas_call(functools.partial(kernel, sizes), out_shape=(jax.ShapeDtyp...  57 us

profile of v4, /device:TPU:1, one launch (start us, length us, event | category | flops | bytes accessed | tf_op | source)
XLA Modules:
  0.0 58.7 jit_solution(3700571843538050562)
XLA Ops:
  0.6 57.0 %shard_map.50 = (f32[4,128,512]{2,1,0:T(8,128)S(1)}, f32[1,128]{1,0:T(1,128)S(1)}) custom-call(f32[4,128,512]{2,1,0:T(8,128)} %f_hbm.1, s32[4,128,512]{2,1,0:T(8,128)} %ori_hbm.1, s32[4,128,512]{2,1,0:T(8,128)} %itf_hbm.1), custom_call_target="tpu_custom_call" | custom-call | tf_op jit(solution)/shard_map/pallas_call | solution.py:491
  57.7 1.0 %shard_map.51 = (f32[4,128,512]{2,1,0:T(8,128)}, f32[1,1]{1,0:T(1,128)}) custom-call(f32[4,128,512]{2,1,0:T(8,128)S(1)} %get-tuple-element.6.res, f32[1,128]{1,0:T(1,128)S(1)} %get-tuple-element.7.peak), custom_call_target="tpu_custom_call" | custom-call | tf_op jit(solution)/shard_map/pallas_call | solution.py:527

commit v5 on v4

--- a/solution.py
+++ b/solution.py
@@ -415,7 +415,7 @@
     for d in range(n1 - 1):
         red1(d).start()
     for d in range(n1 - 1):
-        red1(d, -1).wait_recv()
+        red1(n1 - 2 - d, -1).wait_recv()
     r2[me2] = jnp.max(r1[...], axis=0)
     for d in range(n2 - 1):
         red2(d).start()
@@ -462,7 +462,7 @@
     for d in range(n1 - 1):
         red1(d).wait_send()
     for d in range(n2 - 1):
-        red2(d, -1).wait_recv()
+        red2(n2 - 2 - d, -1).wait_recv()
     peak_ref[...] = jnp.max(r2[...], axis=0)
     for d in range(n2 - 1):
         red2(d).wait_send()

time: 58.8 us -> 58.7 us (level)
  no operation moved by 1% of the time
where the time goes in v5:
time: 58.7 us; the launch traced here: 58.6 us
  Pallas kernels  58 us (99%)
  between operations  0.64 us (1%)
    pallas_call x1, Pallas kernels, block(): pl.pallas_call(functools.partial(kernel, sizes), out_shape=(jax.ShapeDtyp...  57 us

profile of v5, /device:TPU:1, one launch (start us, length us, event | category | flops | bytes accessed | tf_op | source)
XLA Modules:
  0.0 58.6 jit_solution(435004736281707079)
XLA Ops:
  0.6 57.0 %shard_map.50 = (f32[4,128,512]{2,1,0:T(8,128)S(1)}, f32[1,128]{1,0:T(1,128)S(1)}) custom-call(f32[4,128,512]{2,1,0:T(8,128)} %f_hbm.1, s32[4,128,512]{2,1,0:T(8,128)} %ori_hbm.1, s32[4,128,512]{2,1,0:T(8,128)} %itf_hbm.1), custom_call_target="tpu_custom_call" | custom-call | tf_op jit(solution)/shard_map/pallas_call | solution.py:491
  57.6 1.0 %shard_map.51 = (f32[4,128,512]{2,1,0:T(8,128)}, f32[1,1]{1,0:T(1,128)}) custom-call(f32[4,128,512]{2,1,0:T(8,128)S(1)} %get-tuple-element.6.res, f32[1,128]{1,0:T(1,128)S(1)} %get-tuple-element.7.peak), custom_call_target="tpu_custom_call" | custom-call | tf_op jit(solution)/shard_map/pallas_call | solution.py:527

commit v6 on v5

--- a/solution.py
+++ b/solution.py
@@ -469,11 +469,11 @@
 
 
 def settle(res, peak, out, peak_out, top, sems):
-    copies = [pltpu.make_async_copy(res.at[p], out.at[p], sems.at[p]) for p in range(res.shape[0])]
+    copies = [pltpu.make_async_copy(res, out, sems.at[0])]
     for copy in copies:
         copy.start()
     top[0, 0] = jnp.max(peak[...])
-    last = pltpu.make_async_copy(top, peak_out, sems.at[res.shape[0]])
+    last = pltpu.make_async_copy(top, peak_out, sems.at[1])
     last.start()
     last.wait()
     for copy in copies:
@@ -532,7 +532,7 @@
         ),
         in_specs=[pl.BlockSpec(memory_space=pltpu.VMEM), pl.BlockSpec(memory_space=pltpu.VMEM)],
         out_specs=(pl.BlockSpec(memory_space=pl.ANY),) * 2,
-        scratch_shapes=[pltpu.SMEM((1, 1), f32), dma((planes + 1,))], compiler_params=pltpu.CompilerParams(vmem_limit_bytes=1048576 * 2),
+        scratch_shapes=[pltpu.SMEM((1, 1), f32), dma((2,))], compiler_params=pltpu.CompilerParams(vmem_limit_bytes=1048576 * 2),
     )(curvature, peak)
     return curvature, peak.reshape(())
 

time: 58.7 us -> 58.7 us (level)
  no operation moved by 1% of the time
where the time goes in v6:
time: 58.7 us; the launch traced here: 58.6 us
  Pallas kernels  58 us (99%)
  between operations  0.64 us (1%)
    pallas_call x1, Pallas kernels, block(): pl.pallas_call(functools.partial(kernel, sizes), out_shape=(jax.ShapeDtyp...  57 us

profile of v6, /device:TPU:1, one launch (start us, length us, event | category | flops | bytes accessed | tf_op | source)
XLA Modules:
  0.0 58.6 jit_solution(1392482785586756798)
XLA Ops:
  0.6 57.0 %shard_map.50 = (f32[4,128,512]{2,1,0:T(8,128)S(1)}, f32[1,128]{1,0:T(1,128)S(1)}) custom-call(f32[4,128,512]{2,1,0:T(8,128)} %f_hbm.1, s32[4,128,512]{2,1,0:T(8,128)} %ori_hbm.1, s32[4,128,512]{2,1,0:T(8,128)} %itf_hbm.1), custom_call_target="tpu_custom_call" | custom-call | tf_op jit(solution)/shard_map/pallas_call | solution.py:491
  57.6 1.0 %shard_map.51 = (f32[4,128,512]{2,1,0:T(8,128)}, f32[1,1]{1,0:T(1,128)}) custom-call(f32[4,128,512]{2,1,0:T(8,128)S(1)} %get-tuple-element.6.res, f32[1,128]{1,0:T(1,128)S(1)} %get-tuple-element.7.peak), custom_call_target="tpu_custom_call" | custom-call | tf_op jit(solution)/shard_map/pallas_call | solution.py:527
